TPU v7x, 128 devices: a whole 4x4x4 slice. The times are simulated.
128 devices in a mesh: row: 8 (over y, core), col: 16 (over x, z).
Axes of the slice: x: 4, y: 4, z: 4, core: 2. Of those that a mesh axis runs over, the one named last changes fastest.
Arguments:
- upper_a: bfloat16 [2, 4096, 8192], P(None, 'row', 'col'), may hold values from -0.125 to 0.125
- upper_b: bfloat16 [4, 4096, 2, 8192], P(None, 'row', None, 'col'), may hold values from -0.125 to 0.125
- right_side: bfloat16 [2, 4096, 2, 8192], P(None, 'row', None, 'col'), may hold values from -6 to 6
- a_bases: bfloat16 [2, 4096, 512], P(None, 'row'), may hold values from -1 to 1, as said below
- b_bases: bfloat16 [2, 8192, 512], P(None, 'col'), may hold values from -1 to 1, as said below
- a_values: float32 [2, 4096], P(None, 'row'), may hold values from 0.25 to 4
- b_values: float32 [2, 8192], P(None, 'col'), may hold values from 0.25 to 4
Outputs:
- solution: float32 [2, 4096, 2, 8192], P(None, 'row', None, 'col')
Inputs may be any that keep to these rules, and one draw needn't show every extreme that they name: Each tile of a_bases is an orthonormal matrix rounded to bfloat16. Each tile of b_bases is an orthonormal matrix rounded to bfloat16.
All inputs are finite; a program needn't handle non-finite values.
Results may differ from a plain program's by a relative error of at most 0.012.
Values may be sent and summed in bfloat16 or wider, within the bound.
A program may use at most 128 MiB of HBM per device.

v0:
```python
import jax
import jax.numpy as jnp
from jax import lax
from jax.sharding import PartitionSpec as P

FRONTS = 4


def passed_along(block, axis, distance):
    devices = range(lax.axis_size(axis))
    route = [((i - distance) % len(devices), i) for i in devices]
    return lax.ppermute(block, axis, route)


def broadcast(value, axis, root):
    return lax.dynamic_index_in_dim(lax.all_gather(value, axis), root, 0, keepdims=False)


def spread(block, axis, holder):
    block = jnp.where(lax.axis_index(axis) == holder, block, jnp.zeros_like(block))
    return lax.psum(block, axis)


def solve_tile(waiting, basis_left, values_left, basis_right, values_right):
    rounded = waiting.astype(jnp.bfloat16)
    first_half = lax.dot_general(
        basis_left, rounded, (((0,), (0,)), ((), ())), preferred_element_type=jnp.float32
    ).astype(jnp.bfloat16)
    scaled = jnp.dot(first_half, basis_right, preferred_element_type=jnp.float32)
    scaled = (scaled / (values_left[:, None] + values_right[None, :])).astype(jnp.bfloat16)
    left_side = jnp.dot(basis_left, scaled, preferred_element_type=jnp.float32).astype(jnp.bfloat16)
    return lax.dot_general(
        left_side, basis_right, (((1,), (1,)), ((), ())), preferred_element_type=jnp.float32
    ).astype(jnp.bfloat16)


def skip_tile(waiting, basis_left, values_left, basis_right, values_right):
    return jnp.zeros(waiting.shape, jnp.bfloat16)


def shift_columns(block, offset):
    return passed_along(block, "col", offset)


def shift_used(block, offset):
    return passed_along(block, "row", offset)


def shards(upper_a, upper_b, right_side, a_bases, b_bases, a_values, b_values):
    row_count = lax.axis_size("row")
    col_count = lax.axis_size("col")
    row_id = lax.axis_index("row")
    col_id = lax.axis_index("col")
    tile_rows = right_side.shape[0]
    tile_cols = right_side.shape[2]
    b_local_rows = upper_b.shape[0]
    first_front = col_count - 2
    rows_glob = jnp.arange(tile_rows, dtype=jnp.int32) * row_count + row_id
    cols_glob = jnp.arange(tile_cols, dtype=jnp.int32) * col_count + col_id
    working = right_side.astype(jnp.float32)
    a_blocks = []
    for front_step in range(FRONTS):
        if front_step == 1:
            a_blocks.append(upper_a)
        else:
            a_blocks.append(shift_columns(upper_a, front_step - 1))
    b_blocks = []
    for front_step in range(FRONTS):
        target_row = (row_id + 1 - front_step) % row_count
        target_glob = jnp.arange(tile_rows, dtype=jnp.int32) * row_count + target_row
        picks = jnp.clip((front_step - 1 + target_glob) // row_count, 0, b_local_rows - 1)
        chosen = jnp.take(upper_b, picks, axis=0)
        if front_step == 1:
            b_blocks.append(chosen)
        else:
            b_blocks.append(shift_used(chosen, 1 - front_step))
    front_of = (col_count - 1 - rows_glob)[:, None] + cols_glob[None, :]
    for front_step in range(FRONTS):
        front_id = first_front + front_step
        owned = front_of == front_id
        holder = jnp.any(owned)
        flat_index = jnp.argmax(owned.reshape(-1).astype(jnp.int32))
        a_pick = flat_index // tile_cols
        b_pick = flat_index % tile_cols
        waiting = working[a_pick, :, b_pick, :]
        x_tile = lax.cond(
            holder,
            solve_tile,
            skip_tile,
            waiting,
            a_bases[a_pick],
            a_values[a_pick],
            b_bases[b_pick],
            b_values[b_pick],
        )
        working = working.at[a_pick, :, b_pick, :].set(
            jnp.where(holder, x_tile.astype(jnp.float32), waiting)
        )
        column_x = broadcast(x_tile, "row", (1 - front_step + col_id) % row_count)
        row_list = []
        for row_part in range(tile_rows):
            root_col = (front_step - 1 + row_part * row_count + row_id) % col_count
            row_list.append(spread(x_tile, "col", root_col))
        row_x = jnp.stack(row_list)
        k_glob = col_count - 1 - front_id + cols_glob
        k_valid = (k_glob >= 0) & (k_glob <= col_count - 1)
        column_mask = (k_valid[None, :] & (rows_glob[:, None] < k_glob[None, :])).astype(
            jnp.float32
        )
        column_terms = jnp.einsum(
            "apq,qr->apr", a_blocks[front_step], column_x, preferred_element_type=jnp.float32
        )
        l_glob = front_id - col_count + 1 + rows_glob
        row_mask = ((l_glob[:, None] >= 0) & (l_glob[:, None] < cols_glob[None, :])).astype(
            jnp.float32
        )
        row_terms = jnp.einsum(
            "apq,aqbr->apbr", row_x, b_blocks[front_step], preferred_element_type=jnp.float32
        )
        working = (
            working
            - column_terms[:, :, None, :] * column_mask[:, None, :, None]
            - row_terms * row_mask[:, None, :, None]
        )
    return working


def solution(mesh):
    return jax.shard_map(
        shards,
        mesh=mesh,
        in_specs=(
            P(None, "row", "col"),
            P(None, "row", None, "col"),
            P(None, "row", None, "col"),
            P(None, "row", None),
            P(None, "col", None),
            P(None, "row"),
            P(None, "col"),
        ),
        out_specs=P(None, "row", None, "col"),
        check_vma=False,
    )
```

profile of v0, /device:TPU:0, one launch (start us, length us, event | category | flops | bytes accessed | tf_op | source)
XLA Modules:
  0.0 492.8 jit_solution(4523634216439111667)
XLA Ops:
  7.5 0.8 and_convert_fusion.1
  11.5 4.3 copy_convert_fusion
  16.5 2.3 dynamic-slice_bitcast_fusion.3
  18.9 0.8 copy-done.2
  19.8 7.0 %gather_fusion = bf16[2,512,2,512]{3,2,1,0:T(2,128)(2,1)S(1)} fusion(bf16[4,512,2,512]{3,2,1,0:T(2,128)(2,1)} %param.26, s32[1024]{0:T(1024)S(1)} %pad_clamp_fusion.3), kind=kCustom, calls=%fused_computation.clone | custom fusion | bytes 4194312 | tf_op jit(solution)/shard_map/jit(_take)/gather | solution.py:72
  26.9 1.7 copy_select_fusion.2
  28.6 3.0 collective-permute-start.1
  31.5 3.4 collective-permute-start
  34.9 1.1 select_bitcast_fusion.7
  36.1 0.7 iota_reduce_fusion.2
  39.9 0.7 and_reduce_fusion.2
  40.7 3.9 fusion.88
  44.6 17.6 %collective-permute-done = bf16[2,512,512]{2,1,0:T(8,128)(2,1)S(1)} collective-permute-done((bf16[2,512,512]{2,1,0:T(8,128)(2,1)}, bf16[2,512,512]{2,1,0:T(8,128)(2,1)S(1)}, u32[]{:S(2)}, u32[]{:S(2)}) %collective-permute-start) | collective-permute-done | bytes 1048608 | tf_op jit(solution)/shard_map/ppermute | solution.py:12
  62.3 4.6 all-gather.9.cloned.1.call-done
  66.8 3.2 convolution_bitcast_fusion.3
  70.0 1.9 copy.21
  71.9 59.6 %all-reduce.15.cloned.1.call-done = (bf16[1,512,512]{2,1,0:T(8,128)(2,1)}, bf16[1,512,512]{2,1,0:T(8,128)(2,1)}) async-done(((bf16[1,512,512]{2,1,0:T(8,128)(2,1)}, bf16[1,512,512]{2,1,0:T(8,128)(2,1)}), (bf16[1,512,512]{2,1,0:T(8,128)(2,1)}, bf16[1,512,512]{2,1,0:T(8,128)(2,1)})) %all-reduce.15.cloned.1.call-update) | async-done | bytes 1048592 | tf_op jit(solution)/shard_map/psum | solution.py:21
  131.5 6.5 %multiply_subtract_fusion.3 = f32[2,512,2,512]{3,1,2,0:T(8,128)} fusion(f32[2,512,2,512]{3,1,2,0:T(8,128)} %fusion.88, bf16[2,512,2,512]{3,1,2,0:T(8,128)(2,1)} %collective-permute-done.1, f32[2,2]{1,0:T(2,128)S(1)} %get-tuple-element.403, f32[2,2]{1,0:T(2,128)S(1)} %get-tuple-element.390, f32[2,512,512]{2,1,0:T(8,128)S(1)} %copy.21, ...), kind=kOutput, calls=%fused_computation.79 | convolution fusion | flops 1080033280 | bytes 13631520 | tf_op jit(solution)/shard_map/apq,aqbr->apbr/dot_general | solution.py:117
  138.0 2.4 dynamic-slice_bitcast_fusion.2
  140.5 2.7 conditional.5
  140.5 2.0 fusion.19
  142.5 0.7 convolution_convert_fusion.3
  143.2 0.8 copy-done.4
  147.6 8.0 %gather_fusion.1 = bf16[2,512,2,512]{3,2,1,0:T(2,128)(2,1)} fusion(bf16[4,512,2,512]{3,2,1,0:T(2,128)(2,1)} %param.26, s32[1024]{0:T(1024)S(1)} %pad_clamp_fusion.2), kind=kCustom, calls=%fused_computation.1.clone | custom fusion | bytes 4194312 | tf_op jit(solution)/shard_map/jit(_take)/gather | solution.py:72
  156.1 1.1 select_bitcast_fusion.5
  157.2 3.5 broadcast_select_fusion
  160.7 3.7 fusion.87
  164.4 10.4 %all-gather.11.cloned.1.call-done = bf16[4096,512]{1,0:T(8,128)(2,1)} async-done(((bf16[512,512]{1,0:T(8,128)(2,1)}), bf16[4096,512]{1,0:T(8,128)(2,1)}) %all-gather.11.cloned.1.call-update) | async-done | bytes 4194320 | tf_op jit(solution)/shard_map/all_gather | solution.py:16
  174.9 3.5 convolution_bitcast_fusion.2
  178.4 2.9 copy.24
  181.3 61.7 %all-reduce.13.cloned.1.call-done = (bf16[1,512,512]{2,1,0:T(8,128)(2,1)}, bf16[1,512,512]{2,1,0:T(8,128)(2,1)}) async-done(((bf16[1,512,512]{2,1,0:T(8,128)(2,1)}, bf16[1,512,512]{2,1,0:T(8,128)(2,1)}), (bf16[1,512,512]{2,1,0:T(8,128)(2,1)}, bf16[1,512,512]{2,1,0:T(8,128)(2,1)})) %all-reduce.13.cloned.1.call-update) | async-done | bytes 1048592 | tf_op jit(solution)/shard_map/psum | solution.py:21
  243.0 4.6 multiply_subtract_fusion.2
  247.6 2.0 copy-done
  249.6 1.1 dynamic-slice_bitcast_fusion.1
  251.3 0.8 copy-done.6
  252.2 7.0 %gather_fusion.2 = bf16[2,512,2,512]{3,2,1,0:T(2,128)(2,1)S(1)} fusion(bf16[4,512,2,512]{3,2,1,0:T(2,128)(2,1)} %param.26, s32[1024]{0:T(1024)S(1)} %pad_clamp_fusion.1), kind=kCustom, calls=%fused_computation.2.clone | custom fusion | bytes 4194312 | tf_op jit(solution)/shard_map/jit(_take)/gather | solution.py:72
  259.3 1.7 copy_select_fusion.1
  261.0 3.9 collective-permute-start.3
  265.0 0.9 collective-permute-start.2
  265.9 1.1 select_bitcast_fusion.3
  271.1 0.7 and_reduce_fusion
  271.9 4.1 fusion.86
  276.0 18.3 %collective-permute-done.2 = bf16[2,512,512]{2,1,0:T(8,128)(2,1)S(1)} collective-permute-done((bf16[2,512,512]{2,1,0:T(8,128)(2,1)}, bf16[2,512,512]{2,1,0:T(8,128)(2,1)S(1)}, u32[]{:S(2)}, u32[]{:S(2)}) %collective-permute-start.2) | collective-permute-done | bytes 1048608 | tf_op jit(solution)/shard_map/ppermute | solution.py:12
  294.4 3.2 convolution_bitcast_fusion.1
  297.5 1.9 copy.27
  299.4 4.8 collective-permute-done.3
  304.2 55.2 %all-reduce.11.cloned.1.call-done = (bf16[1,512,512]{2,1,0:T(8,128)(2,1)}, bf16[1,512,512]{2,1,0:T(8,128)(2,1)}) async-done(((bf16[1,512,512]{2,1,0:T(8,128)(2,1)}, bf16[1,512,512]{2,1,0:T(8,128)(2,1)}), (bf16[1,512,512]{2,1,0:T(8,128)(2,1)}, bf16[1,512,512]{2,1,0:T(8,128)(2,1)})) %all-reduce.11.cloned.1.call-update) | async-done | bytes 1048592 | tf_op jit(solution)/shard_map/psum | solution.py:21
  359.4 4.5 multiply_subtract_fusion.1
  364.0 2.0 copy-done.1
  366.0 1.1 dynamic-slice_bitcast_fusion
  367.9 0.8 copy-done.8
  368.8 7.0 %gather_fusion.3 = bf16[2,512,2,512]{3,2,1,0:T(2,128)(2,1)S(1)} fusion(bf16[4,512,2,512]{3,2,1,0:T(2,128)(2,1)} %param.26, s32[1024]{0:T(1024)S(1)} %pad_clamp_fusion), kind=kCustom, calls=%fused_computation.3.clone | custom fusion | bytes 4194312 | tf_op jit(solution)/shard_map/jit(_take)/gather | solution.py:72
  375.9 1.7 copy_select_fusion
  377.6 5.5 %collective-permute-start.5 = (bf16[2,512,2,512]{3,1,2,0:T(8,128)(2,1)}, bf16[2,512,2,512]{3,1,2,0:T(8,128)(2,1)}, u32[]{:S(2)}, u32[]{:S(2)}) collective-permute-start(bf16[2,512,2,512]{3,1,2,0:T(8,128)(2,1)} %copy_select_fusion), channel_id=1, source_target_pairs={{32,0},{48,16},{64,32},{80,48},{96,64},{112,80},{0,96},{16,112},{3... | collective-permute-start | bytes 6291464 | tf_op jit(solution)/shard_map/ppermute | solution.py:12
  383.1 1.1 select_bitcast_fusion.1
  384.2 4.0 fusion.85
  388.2 22.6 %collective-permute-done.4 = bf16[2,512,512]{2,1,0:T(8,128)(2,1)S(1)} collective-permute-done((bf16[2,512,512]{2,1,0:T(8,128)(2,1)}, bf16[2,512,512]{2,1,0:T(8,128)(2,1)S(1)}, u32[]{:S(2)}, u32[]{:S(2)}) %collective-permute-start.4) | collective-permute-done | bytes 1048608 | tf_op jit(solution)/shard_map/ppermute | solution.py:12
  410.9 7.6 %all-gather.15.cloned.1.call-done = bf16[4096,512]{1,0:T(8,128)(2,1)} async-done(((bf16[512,512]{1,0:T(8,128)(2,1)}), bf16[4096,512]{1,0:T(8,128)(2,1)}) %all-gather.15.cloned.1.call-update) | async-done | bytes 4194320 | tf_op jit(solution)/shard_map/all_gather | solution.py:16
  418.5 3.2 convolution_bitcast_fusion
  421.6 1.9 copy.30
  423.6 16.7 %collective-permute-done.5 = bf16[2,512,2,512]{3,1,2,0:T(8,128)(2,1)} collective-permute-done((bf16[2,512,2,512]{3,1,2,0:T(8,128)(2,1)}, bf16[2,512,2,512]{3,1,2,0:T(8,128)(2,1)}, u32[]{:S(2)}, u32[]{:S(2)}) %collective-permute-start.5) | collective-permute-done | bytes 2097184 | tf_op jit(solution)/shard_map/ppermute | solution.py:12
  440.3 35.4 %all-reduce.9.cloned.1.call-done = (bf16[1,512,512]{2,1,0:T(8,128)(2,1)}, bf16[1,512,512]{2,1,0:T(8,128)(2,1)}) async-done(((bf16[1,512,512]{2,1,0:T(8,128)(2,1)}, bf16[1,512,512]{2,1,0:T(8,128)(2,1)}), (bf16[1,512,512]{2,1,0:T(8,128)(2,1)}, bf16[1,512,512]{2,1,0:T(8,128)(2,1)})) %all-reduce.9.cloned.1.call-update) | async-done | bytes 1048592 | tf_op jit(solution)/shard_map/psum | solution.py:21
  475.6 4.5 multiply_subtract_fusion
  480.2 5.2 %copy.32 = f32[2,512,2,512]{3,2,1,0:T(2,128)} copy(f32[2,512,2,512]{3,1,2,0:T(8,128)S(1)} %multiply_subtract_fusion) | data formatting | bytes 8388608 | tf_op jit(solution)/shard_map/sub | solution.py:121
  (83 shorter events, 5.0 us)
Async XLA Ops:
  7.4 59.5 %all-gather.9.cloned.1.call-start = ((), (), s32[]{:S(2)}) async-start(), calls=%async_computation | async-start | bytes 4718592 | tf_op jit(solution)/shard_map/all_gather | solution.py:16
  15.8 3.0 copy-start.10
  15.8 3.0 copy-start.11
  15.8 3.0 copy-start.13
  18.9 0.8 copy-start.2
  19.7 111.8 %all-reduce.15.cloned.1.call-start = ((), (), s32[]{:S(2)}) async-start(), calls=%async_computation.7 | async-start | bytes 2097152 | tf_op jit(solution)/shard_map/psum | solution.py:21
  26.8 8.1 %copy-start.3 = (bf16[512,512]{1,0:T(8,128)(2,1)S(1)}, bf16[512,512]{1,0:T(8,128)(2,1)}, u32[]{:S(2)}) copy-start(bf16[512,512]{1,0:T(8,128)(2,1)} %copy-done.2) | copy-start | bytes 1572868
  28.6 11.4 %copy-start.12 = (s32[4]{0:T(128)S(1)}, s32[4]{0:T(128)}, u32[]{:S(2)}) copy-start(s32[4]{0:T(128)} %constant.378.clone.1) | copy-start | bytes 52
  28.6 103.0 %collective-permute-start.1 = (bf16[2,512,2,512]{3,1,2,0:T(8,128)(2,1)}, bf16[2,512,2,512]{3,1,2,0:T(8,128)(2,1)}, u32[]{:S(2)}, u32[]{:S(2)}) collective-permute-start(bf16[2,512,2,512]{3,1,2,0:T(8,128)(2,1)} %copy_select_fusion.2), channel_id=1, source_target_pairs={{112,0},{0,16},{16,32},{32,48},{48,64},{64,80},{80,96},{96,112},{1... | collective-permute-start | bytes 6291464 | tf_op jit(solution)/shard_map/ppermute | solution.py:12
  31.5 30.7 %collective-permute-start = (bf16[2,512,512]{2,1,0:T(8,128)(2,1)}, bf16[2,512,512]{2,1,0:T(8,128)(2,1)S(1)}, u32[]{:S(2)}, u32[]{:S(2)}) collective-permute-start(bf16[2,512,512]{2,1,0:T(8,128)(2,1)} %param.25), channel_id=1, source_target_pairs={{1,0},{2,1},{3,2},{4,3},{5,4},{6,5},{7,6},{8,7},{9,8},{10,9},{11,1... | collective-permute-start | bytes 3145736 | tf_op jit(solution)/shard_map/ppermute | solution.py:12
  36.0 138.9 %all-gather.11.cloned.1.call-start = ((), (), s32[]{:S(2)}) async-start(), calls=%async_computation.1 | async-start | bytes 4718592 | tf_op jit(solution)/shard_map/all_gather | solution.py:16
  138.0 2.4 copy-start.14
  138.0 2.4 copy-start.17
  143.2 0.8 copy-start.4
  144.0 99.0 %all-reduce.13.cloned.1.call-start = ((), (), s32[]{:S(2)}) async-start(), calls=%async_computation.6 | async-start | bytes 2097152 | tf_op jit(solution)/shard_map/psum | solution.py:21
  147.5 8.6 %copy-start.5 = (bf16[512,512]{1,0:T(8,128)(2,1)S(1)}, bf16[512,512]{1,0:T(8,128)(2,1)}, u32[]{:S(2)}) copy-start(bf16[512,512]{1,0:T(8,128)(2,1)} %copy-done.4) | copy-start | bytes 1572868
  157.2 137.2 %all-gather.13.cloned.1.call-start = ((), (), s32[]{:S(2)}) async-start(), calls=%async_computation.2 | async-start | bytes 4718592 | tf_op jit(solution)/shard_map/all_gather | solution.py:16
  247.6 2.0 copy-start
  249.6 1.6 copy-start.15
  251.3 0.8 copy-start.6
  252.1 107.3 %all-reduce.11.cloned.1.call-start = ((), (), s32[]{:S(2)}) async-start(), calls=%async_computation.5 | async-start | bytes 2097152 | tf_op jit(solution)/shard_map/psum | solution.py:21
  259.3 6.6 %copy-start.7 = (bf16[512,512]{1,0:T(8,128)(2,1)S(1)}, bf16[512,512]{1,0:T(8,128)(2,1)}, u32[]{:S(2)}) copy-start(bf16[512,512]{1,0:T(8,128)(2,1)} %copy-done.6) | copy-start | bytes 1572868
  261.0 43.2 %collective-permute-start.3 = (bf16[2,512,2,512]{3,1,2,0:T(8,128)(2,1)}, bf16[2,512,2,512]{3,1,2,0:T(8,128)(2,1)}, u32[]{:S(2)}, u32[]{:S(2)}) collective-permute-start(bf16[2,512,2,512]{3,1,2,0:T(8,128)(2,1)} %copy_select_fusion.1), channel_id=1, source_target_pairs={{16,0},{32,16},{48,32},{64,48},{80,64},{96,80},{112,96},{0,112},{1... | collective-permute-start | bytes 6291464 | tf_op jit(solution)/shard_map/ppermute | solution.py:12
  265.0 29.4 %collective-permute-start.2 = (bf16[2,512,512]{2,1,0:T(8,128)(2,1)}, bf16[2,512,512]{2,1,0:T(8,128)(2,1)S(1)}, u32[]{:S(2)}, u32[]{:S(2)}) collective-permute-start(bf16[2,512,512]{2,1,0:T(8,128)(2,1)} %param.25), channel_id=1, source_target_pairs={{15,0},{0,1},{1,2},{2,3},{3,4},{4,5},{5,6},{6,7},{7,8},{8,9},{9,10... | collective-permute-start | bytes 3145736 | tf_op jit(solution)/shard_map/ppermute | solution.py:12
  267.0 151.5 %all-gather.15.cloned.1.call-start = ((), (), s32[]{:S(2)}) async-start(), calls=%async_computation.3 | async-start | bytes 4718592 | tf_op jit(solution)/shard_map/all_gather | solution.py:16
  363.9 2.0 copy-start.1
  366.0 1.6 copy-start.16
  366.0 1.9 copy-start.18
  367.9 0.8 copy-start.8
  368.7 106.9 %all-reduce.9.cloned.1.call-start = ((), (), s32[]{:S(2)}) async-start(), calls=%async_computation.4 | async-start | bytes 2097152 | tf_op jit(solution)/shard_map/psum | solution.py:21
  375.9 7.2 %copy-start.9 = (bf16[512,512]{1,0:T(8,128)(2,1)S(1)}, bf16[512,512]{1,0:T(8,128)(2,1)}, u32[]{:S(2)}) copy-start(bf16[512,512]{1,0:T(8,128)(2,1)} %copy-done.8) | copy-start | bytes 1572868
  377.6 62.7 %collective-permute-start.5 = (bf16[2,512,2,512]{3,1,2,0:T(8,128)(2,1)}, bf16[2,512,2,512]{3,1,2,0:T(8,128)(2,1)}, u32[]{:S(2)}, u32[]{:S(2)}) collective-permute-start(bf16[2,512,2,512]{3,1,2,0:T(8,128)(2,1)} %copy_select_fusion), channel_id=1, source_target_pairs={{32,0},{48,16},{64,32},{80,48},{96,64},{112,80},{0,96},{16,112},{3... | collective-permute-start | bytes 6291464 | tf_op jit(solution)/shard_map/ppermute | solution.py:12
  383.1 27.8 %collective-permute-start.4 = (bf16[2,512,512]{2,1,0:T(8,128)(2,1)}, bf16[2,512,512]{2,1,0:T(8,128)(2,1)S(1)}, u32[]{:S(2)}, u32[]{:S(2)}) collective-permute-start(bf16[2,512,512]{2,1,0:T(8,128)(2,1)} %param.25), channel_id=1, source_target_pairs={{14,0},{15,1},{0,2},{1,3},{2,4},{3,5},{4,6},{5,7},{6,8},{7,9},{8,1... | collective-permute-start | bytes 3145736 | tf_op jit(solution)/shard_map/ppermute | solution.py:12
Sparse Core Ops, SparseCore 0:
  19.8 46.9 all-gather.8
  144.1 30.7 all-gather.10
  252.2 41.5 all-gather.12
  368.9 49.5 all-gather.14
Sparse Core Ops, SparseCore 1:
  36.1 95.4 all-reduce.14
  157.3 85.7 all-reduce.12
  267.1 92.3 all-reduce.10
  384.3 91.3 all-reduce.8
where the time goes:
time: 494 us; the launch traced here: 493 us
  waiting for transfers between devices  315 us (64%)
  local copies, waits for them, and re-layouts  58.9 us (12%)
  other arithmetic  38.2 us (8%)
  matrix products  35.8 us (7%)
  between operations  27.7 us (6%)
  starting transfers between devices  17.4 us (4%)
    psum x4, waiting for transfers between devices, spread(): return lax.psum(block, axis)  212 us
    ppermute x6, waiting for transfers between devices, passed_along(): return lax.ppermute(block, axis, route)  80.1 us
    gather x4, local copies, waits for them, and re-layouts, shards(): chosen = jnp.take(upper_b, picks, axis=0)  29.1 us
    all_gather x4, waiting for transfers between devices, broadcast(): lax.all_gather(value, axis)  22.6 us
    dot_general x4, matrix products, shards(): jnp.einsum('apq,aqbr->apbr', row_x, b_blocks[front_step], preferred_eleme...  20.2 us
    ppermute x6, starting transfers between devices, passed_along(): return lax.ppermute(block, axis, route)  16.7 us
    scatter x4, other arithmetic, shards(): working.at[a_pick, :, b_pick, :]  15.9 us
    dot_general x4, matrix products, shards(): jnp.einsum('apq,qr->apr', a_blocks[front_step], column_x, preferred_eleme...  12.9 us
  transfers between devices with their start and end apart: 14, of which 12 were waited for; matrix products, arithmetic and copies ran while one was open for 17% of the time, Pallas kernels for 0%

commit v1 on v0

--- a/solution.py
+++ b/solution.py
@@ -18,7 +18,7 @@
 
 def spread(block, axis, holder):
     block = jnp.where(lax.axis_index(axis) == holder, block, jnp.zeros_like(block))
-    return lax.psum(block, axis)
+    return jnp.sum(lax.all_gather(block, axis), axis=0)
 
 
 def solve_tile(waiting, basis_left, values_left, basis_right, values_right):

time: 494 us -> 850 us (1.72); the launches traced: 493 us -> 840 us
  waiting for transfers between devices: 315 us -> 619 us
  other arithmetic: 38.2 us -> 81.3 us
    all_gather x0 -> x8, waiting for transfers between devices: none -> 543 us  [spread(): return jnp.sum(lax.all_gather(block, axis), axis=0)]
    psum x4 -> x0, waiting for transfers between devices: 212 us -> none  [spread(): return lax.psum(block, axis)]
    reduce_sum x0 -> x8, other arithmetic: none -> 38.6 us  [spread(): return jnp.sum(lax.all_gather(block, axis), axis=0)]
    ppermute x6, waiting for transfers between devices: 80.1 us -> 49.3 us  [passed_along(): return lax.ppermute(block, axis, route)]
  transfers between devices with their start and end apart: 14 -> 18, of which waited for: 12 -> 15; matrix products, arithmetic and copies ran while one was open for 17% -> 14% of each run, Pallas kernels for 0% -> 0%
where the time goes in v1:
time: 850 us; the launch traced here: 840 us
  waiting for transfers between devices  619 us (73%)
  other arithmetic  81.3 us (10%)
  local copies, waits for them, and re-layouts  57.9 us (7%)
  matrix products  35 us (4%)
  between operations  26.8 us (3%)
  starting transfers between devices  19.1 us (2%)
    all_gather x8, waiting for transfers between devices, spread(): return jnp.sum(lax.all_gather(block, axis), axis=0)  543 us
    ppermute x6, waiting for transfers between devices, passed_along(): return lax.ppermute(block, axis, route)  49.3 us
    reduce_sum x8, other arithmetic, spread(): return jnp.sum(lax.all_gather(block, axis), axis=0)  38.6 us
    gather x4, local copies, waits for them, and re-layouts, shards(): chosen = jnp.take(upper_b, picks, axis=0)  29.3 us
    all_gather x4, waiting for transfers between devices, broadcast(): lax.all_gather(value, axis)  25.1 us
    dot_general x4, matrix products, shards(): jnp.einsum('apq,aqbr->apbr', row_x, b_blocks[front_step], preferred_eleme...  18.9 us
    ppermute x6, starting transfers between devices, passed_along(): return lax.ppermute(block, axis, route)  18.5 us
  transfers between devices with their start and end apart: 18, of which 15 were waited for; matrix products, arithmetic and copies ran while one was open for 14% of the time, Pallas kernels for 0%

profile of v1, /device:TPU:0, one launch (start us, length us, event | category | flops | bytes accessed | tf_op | source)
XLA Modules:
  0.0 840.1 jit_solution(12779200254105849636)
XLA Ops:
  10.6 4.4 copy_convert_fusion
  15.6 2.4 dynamic-slice_bitcast_fusion.3
  19.0 2.1 broadcast_select_fusion.8
  22.0 7.1 gather_fusion
  29.1 1.7 copy_select_fusion.2
  30.8 3.6 collective-permute-start.1
  34.4 2.7 collective-permute-start
  42.1 4.0 fusion.88
  46.0 14.2 %collective-permute-done = bf16[2,512,512]{2,1,0:T(8,128)(2,1)S(1)} collective-permute-done((bf16[2,512,512]{2,1,0:T(8,128)(2,1)}, bf16[2,512,512]{2,1,0:T(8,128)(2,1)S(1)}, u32[]{:S(2)}, u32[]{:S(2)}) %collective-permute-start) | collective-permute-done | bytes 1048608 | tf_op jit(solution)/shard_map/ppermute | solution.py:12
  60.3 6.4 all-gather.25.cloned.1.call-done
  66.6 3.2 convolution_bitcast_fusion.3
  69.8 1.9 copy.21
  71.8 67.1 %all-gather.27.cloned.1.call-done = bf16[8192,512]{1,0:T(8,128)(2,1)} async-done(((bf16[512,512]{1,0:T(8,128)(2,1)}), bf16[8192,512]{1,0:T(8,128)(2,1)}) %all-gather.27.cloned.1.call-update) | async-done | bytes 8388624 | tf_op jit(solution)/shard_map/all_gather | solution.py:21
  138.8 4.8 reduce_sum.96
  143.7 67.9 %all-gather.29.cloned.1.call-done = bf16[8192,512]{1,0:T(8,128)(2,1)} async-done(((bf16[512,512]{1,0:T(8,128)(2,1)}), bf16[8192,512]{1,0:T(8,128)(2,1)}) %all-gather.29.cloned.1.call-update) | async-done | bytes 8388624 | tf_op jit(solution)/shard_map/all_gather | solution.py:21
  211.5 4.8 reduce_sum.97
  216.4 6.2 multiply_subtract_fusion.3
  222.6 2.3 dynamic-slice_bitcast_fusion.2
  224.9 3.6 conditional.5
  225.3 2.4 fusion.19
  229.4 2.1 broadcast_select_fusion.6
  235.2 8.0 gather_fusion.1
  243.9 3.5 broadcast_select_fusion
  247.5 3.8 fusion.87
  251.2 9.4 %all-gather.31.cloned.1.call-done = bf16[4096,512]{1,0:T(8,128)(2,1)} async-done(((bf16[512,512]{1,0:T(8,128)(2,1)}), bf16[4096,512]{1,0:T(8,128)(2,1)}) %all-gather.31.cloned.1.call-update) | async-done | bytes 4194320 | tf_op jit(solution)/shard_map/all_gather | solution.py:16
  260.6 3.5 convolution_bitcast_fusion.2
  264.1 2.9 copy.24
  267.0 66.5 %all-gather.33.cloned.1.call-done = bf16[8192,512]{1,0:T(8,128)(2,1)} async-done(((bf16[512,512]{1,0:T(8,128)(2,1)}), bf16[8192,512]{1,0:T(8,128)(2,1)}) %all-gather.33.cloned.1.call-update) | async-done | bytes 8388624 | tf_op jit(solution)/shard_map/all_gather | solution.py:21
  333.5 4.8 reduce_sum.98
  338.3 67.7 %all-gather.35.cloned.1.call-done = bf16[8192,512]{1,0:T(8,128)(2,1)} async-done(((bf16[512,512]{1,0:T(8,128)(2,1)}), bf16[8192,512]{1,0:T(8,128)(2,1)}) %all-gather.35.cloned.1.call-update) | async-done | bytes 8388624 | tf_op jit(solution)/shard_map/all_gather | solution.py:21
  406.0 4.8 reduce_sum.99
  410.9 4.3 multiply_subtract_fusion.2
  415.2 2.0 copy-done
  417.2 1.1 dynamic-slice_bitcast_fusion.1
  419.5 2.1 broadcast_select_fusion.4
  422.5 7.1 gather_fusion.2
  429.6 1.7 copy_select_fusion.1
  431.3 6.1 collective-permute-start.3
  442.2 4.2 fusion.86
  446.3 14.0 %collective-permute-done.2 = bf16[2,512,512]{2,1,0:T(8,128)(2,1)S(1)} collective-permute-done((bf16[2,512,512]{2,1,0:T(8,128)(2,1)}, bf16[2,512,512]{2,1,0:T(8,128)(2,1)S(1)}, u32[]{:S(2)}, u32[]{:S(2)}) %collective-permute-start.2) | collective-permute-done | bytes 1048608 | tf_op jit(solution)/shard_map/ppermute | solution.py:12
  460.4 1.4 all-gather.37.cloned.1.call-done
  461.8 3.2 convolution_bitcast_fusion.1
  465.0 1.9 copy.27
  466.9 69.0 %all-gather.39.cloned.1.call-done = bf16[8192,512]{1,0:T(8,128)(2,1)} async-done(((bf16[512,512]{1,0:T(8,128)(2,1)}), bf16[8192,512]{1,0:T(8,128)(2,1)}) %all-gather.39.cloned.1.call-update) | async-done | bytes 8388624 | tf_op jit(solution)/shard_map/all_gather | solution.py:21
  535.9 4.8 reduce_sum.100
  540.7 67.9 %all-gather.41.cloned.1.call-done = bf16[8192,512]{1,0:T(8,128)(2,1)} async-done(((bf16[512,512]{1,0:T(8,128)(2,1)}), bf16[8192,512]{1,0:T(8,128)(2,1)}) %all-gather.41.cloned.1.call-update) | async-done | bytes 8388624 | tf_op jit(solution)/shard_map/all_gather | solution.py:21
  608.6 4.8 reduce_sum.101
  613.4 4.2 multiply_subtract_fusion.1
  617.6 2.0 copy-done.1
  621.7 2.1 broadcast_select_fusion.2
  624.4 7.1 gather_fusion.3
  631.5 1.7 copy_select_fusion
  633.2 5.9 collective-permute-start.5
  639.2 4.0 fusion.85
  643.3 21.0 %collective-permute-done.4 = bf16[2,512,512]{2,1,0:T(8,128)(2,1)S(1)} collective-permute-done((bf16[2,512,512]{2,1,0:T(8,128)(2,1)}, bf16[2,512,512]{2,1,0:T(8,128)(2,1)S(1)}, u32[]{:S(2)}, u32[]{:S(2)}) %collective-permute-start.4) | collective-permute-done | bytes 1048608 | tf_op jit(solution)/shard_map/ppermute | solution.py:12
  664.3 7.9 all-gather.43.cloned.1.call-done
  672.2 3.2 convolution_bitcast_fusion
  675.4 1.9 copy.30
  677.3 69.0 %all-gather.45.cloned.1.call-done = bf16[8192,512]{1,0:T(8,128)(2,1)} async-done(((bf16[512,512]{1,0:T(8,128)(2,1)}), bf16[8192,512]{1,0:T(8,128)(2,1)}) %all-gather.45.cloned.1.call-update) | async-done | bytes 8388624 | tf_op jit(solution)/shard_map/all_gather | solution.py:21
  746.2 4.8 reduce_sum.102
  751.1 67.7 %all-gather.47.cloned.1.call-done = bf16[8192,512]{1,0:T(8,128)(2,1)} async-done(((bf16[512,512]{1,0:T(8,128)(2,1)}), bf16[8192,512]{1,0:T(8,128)(2,1)}) %all-gather.47.cloned.1.call-update) | async-done | bytes 8388624 | tf_op jit(solution)/shard_map/all_gather | solution.py:21
  818.8 4.8 reduce_sum.103
  823.6 4.2 multiply_subtract_fusion
  827.8 5.2 copy.32
  (99 shorter events, 14.4 us)
Async XLA Ops:
  6.5 60.1 %all-gather.25.cloned.1.call-start = ((), (), s32[]{:S(2)}) async-start(), calls=%async_computation | async-start | bytes 4718592 | tf_op jit(solution)/shard_map/all_gather | solution.py:16
  10.6 7.4 copy-start.10
  10.6 7.4 copy-start.11
  10.6 7.4 copy-start.13
  10.6 7.4 copy-start.17
  18.1 0.8 copy-start.2
  18.9 120.0 %all-gather.27.cloned.1.call-start = ((), (), s32[]{:S(2)}) async-start(), calls=%async_computation.1 | async-start | bytes 8912896 | tf_op jit(solution)/shard_map/all_gather | solution.py:21
  21.1 190.4 %all-gather.29.cloned.1.call-start = ((), (), s32[]{:S(2)}) async-start(), calls=%async_computation.2 | async-start | bytes 8912896 | tf_op jit(solution)/shard_map/all_gather | solution.py:21
  21.9 238.7 %all-gather.31.cloned.1.call-start = ((), (), s32[]{:S(2)}) async-start(), calls=%async_computation.3 | async-start | bytes 4718592 | tf_op jit(solution)/shard_map/all_gather | solution.py:16
  21.9 19.3 %copy-start.12 = (s32[4]{0:T(128)S(1)}, s32[4]{0:T(128)}, u32[]{:S(2)}) copy-start(s32[4]{0:T(128)} %constant.387.clone.1) | copy-start | bytes 52
  22.0 20.1 %copy-start.3 = (bf16[512,512]{1,0:T(8,128)(2,1)S(1)}, bf16[512,512]{1,0:T(8,128)(2,1)}, u32[]{:S(2)}) copy-start(bf16[512,512]{1,0:T(8,128)(2,1)} %copy-done.2) | copy-start | bytes 1572868
  30.8 185.6 %collective-permute-start.1 = (bf16[2,512,2,512]{3,1,2,0:T(8,128)(2,1)}, bf16[2,512,2,512]{3,1,2,0:T(8,128)(2,1)}, u32[]{:S(2)}, u32[]{:S(2)}) collective-permute-start(bf16[2,512,2,512]{3,1,2,0:T(8,128)(2,1)} %copy_select_fusion.2), channel_id=1, source_target_pairs={{112,0},{0,16},{16,32},{32,48},{48,64},{64,80},{80,96},{96,112},{1... | collective-permute-start | bytes 6291464 | tf_op jit(solution)/shard_map/ppermute | solution.py:12
  34.4 25.9 %collective-permute-start = (bf16[2,512,512]{2,1,0:T(8,128)(2,1)}, bf16[2,512,512]{2,1,0:T(8,128)(2,1)S(1)}, u32[]{:S(2)}, u32[]{:S(2)}) collective-permute-start(bf16[2,512,512]{2,1,0:T(8,128)(2,1)} %param.25), channel_id=1, source_target_pairs={{1,0},{2,1},{3,2},{4,3},{5,4},{6,5},{7,6},{8,7},{9,8},{10,9},{11,1... | collective-permute-start | bytes 3145736 | tf_op jit(solution)/shard_map/ppermute | solution.py:12
  225.3 2.5 copy-start.14
  225.3 2.5 copy-start.18
  228.5 0.8 copy-start.4
  229.4 104.1 %all-gather.33.cloned.1.call-start = ((), (), s32[]{:S(2)}) async-start(), calls=%async_computation.4 | async-start | bytes 8912896 | tf_op jit(solution)/shard_map/all_gather | solution.py:21
  231.5 174.5 %all-gather.35.cloned.1.call-start = ((), (), s32[]{:S(2)}) async-start(), calls=%async_computation.5 | async-start | bytes 8912896 | tf_op jit(solution)/shard_map/all_gather | solution.py:21
  232.1 229.7 %all-gather.37.cloned.1.call-start = ((), (), s32[]{:S(2)}) async-start(), calls=%async_computation.6 | async-start | bytes 4718592 | tf_op jit(solution)/shard_map/all_gather | solution.py:16
  235.2 12.3 %copy-start.5 = (bf16[512,512]{1,0:T(8,128)(2,1)S(1)}, bf16[512,512]{1,0:T(8,128)(2,1)}, u32[]{:S(2)}) copy-start(bf16[512,512]{1,0:T(8,128)(2,1)} %copy-done.4) | copy-start | bytes 1572868
  415.2 2.0 copy-start
  418.6 0.8 copy-start.6
  419.4 116.5 %all-gather.39.cloned.1.call-start = ((), (), s32[]{:S(2)}) async-start(), calls=%async_computation.7 | async-start | bytes 8912896 | tf_op jit(solution)/shard_map/all_gather | solution.py:21
  421.6 187.0 %all-gather.41.cloned.1.call-start = ((), (), s32[]{:S(2)}) async-start(), calls=%async_computation.8 | async-start | bytes 8912896 | tf_op jit(solution)/shard_map/all_gather | solution.py:21
  422.3 249.8 %all-gather.43.cloned.1.call-start = ((), (), s32[]{:S(2)}) async-start(), calls=%async_computation.9 | async-start | bytes 4718592 | tf_op jit(solution)/shard_map/all_gather | solution.py:16
  422.5 19.7 %copy-start.7 = (bf16[512,512]{1,0:T(8,128)(2,1)S(1)}, bf16[512,512]{1,0:T(8,128)(2,1)}, u32[]{:S(2)}) copy-start(bf16[512,512]{1,0:T(8,128)(2,1)} %copy-done.6) | copy-start | bytes 1572868
  431.3 182.1 %collective-permute-start.3 = (bf16[2,512,2,512]{3,1,2,0:T(8,128)(2,1)}, bf16[2,512,2,512]{3,1,2,0:T(8,128)(2,1)}, u32[]{:S(2)}, u32[]{:S(2)}) collective-permute-start(bf16[2,512,2,512]{3,1,2,0:T(8,128)(2,1)} %copy_select_fusion.1), channel_id=1, source_target_pairs={{16,0},{32,16},{48,32},{64,48},{80,64},{96,80},{112,96},{0,112},{1... | collective-permute-start | bytes 6291464 | tf_op jit(solution)/shard_map/ppermute | solution.py:12
  437.4 23.0 %collective-permute-start.2 = (bf16[2,512,512]{2,1,0:T(8,128)(2,1)}, bf16[2,512,512]{2,1,0:T(8,128)(2,1)S(1)}, u32[]{:S(2)}, u32[]{:S(2)}) collective-permute-start(bf16[2,512,512]{2,1,0:T(8,128)(2,1)} %param.25), channel_id=1, source_target_pairs={{15,0},{0,1},{1,2},{2,3},{3,4},{4,5},{5,6},{6,7},{7,8},{8,9},{9,10... | collective-permute-start | bytes 3145736 | tf_op jit(solution)/shard_map/ppermute | solution.py:12
  617.6 2.0 copy-start.1
  620.8 0.8 copy-start.8
  621.6 124.6 %all-gather.45.cloned.1.call-start = ((), (), s32[]{:S(2)}) async-start(), calls=%async_computation.10 | async-start | bytes 8912896 | tf_op jit(solution)/shard_map/all_gather | solution.py:21
  623.8 194.9 %all-gather.47.cloned.1.call-start = ((), (), s32[]{:S(2)}) async-start(), calls=%async_computation.11 | async-start | bytes 8912896 | tf_op jit(solution)/shard_map/all_gather | solution.py:21
  624.4 14.8 %copy-start.9 = (bf16[512,512]{1,0:T(8,128)(2,1)S(1)}, bf16[512,512]{1,0:T(8,128)(2,1)}, u32[]{:S(2)}) copy-start(bf16[512,512]{1,0:T(8,128)(2,1)} %copy-done.8) | copy-start | bytes 1572868
  633.2 190.4 %collective-permute-start.5 = (bf16[2,512,2,512]{3,1,2,0:T(8,128)(2,1)}, bf16[2,512,2,512]{3,1,2,0:T(8,128)(2,1)}, u32[]{:S(2)}, u32[]{:S(2)}) collective-permute-start(bf16[2,512,2,512]{3,1,2,0:T(8,128)(2,1)} %copy_select_fusion), channel_id=1, source_target_pairs={{32,0},{48,16},{64,32},{80,48},{96,64},{112,80},{0,96},{16,112},{3... | collective-permute-start | bytes 6291464 | tf_op jit(solution)/shard_map/ppermute | solution.py:12
  639.1 25.2 %collective-permute-start.4 = (bf16[2,512,512]{2,1,0:T(8,128)(2,1)}, bf16[2,512,512]{2,1,0:T(8,128)(2,1)S(1)}, u32[]{:S(2)}, u32[]{:S(2)}) collective-permute-start(bf16[2,512,512]{2,1,0:T(8,128)(2,1)} %param.25), channel_id=1, source_target_pairs={{14,0},{15,1},{0,2},{1,3},{2,4},{3,5},{4,6},{5,7},{6,8},{7,9},{8,1... | collective-permute-start | bytes 3145736 | tf_op jit(solution)/shard_map/ppermute | solution.py:12
Sparse Core Ops, SparseCore 0:
  19.0 47.5 all-gather.24
  68.8 70.0 all-gather.26
  141.0 70.4 all-gather.28
  229.5 31.0 all-gather.30
  262.6 70.8 all-gather.32
  335.5 70.4 all-gather.34
  419.5 42.2 all-gather.36
  463.9 71.8 all-gather.38
  538.0 70.4 all-gather.40
  621.7 50.3 all-gather.42
  674.3 71.8 all-gather.44
  748.2 70.4 all-gather.46
